TPU v7x, 512 devices: a whole 4x4x16 slice. The times are simulated.
512 devices in a mesh: kvp: 64 (over z, y), tp: 8 (over x, core).
Axes of the slice: x: 4, y: 4, z: 16, core: 2. Of those that a mesh axis runs over, the one named last changes fastest.
Arguments:
- queries: bfloat16 [8, 8192], P(None, 'tp'), may hold values from -12 to 12
- key_pool: bfloat16 [2048, 64, 1024], P('kvp', None, 'tp'), may hold values from -5 to 5
- value_pool: bfloat16 [2048, 64, 1024], P('kvp', None, 'tp'), may hold values from -5 to 5
- block_table: int32 [64, 32], P('kvp'), may hold values from 0 to 31, each once within a row
- lengths: int32 [8], replicated, may hold values from 1 to 16384, 81920 in all
- residual_in: float32 [8, 8192], P(None, 'kvp'), may hold values from -12 to 12
- out_weight: bfloat16 [8192, 8192], P('tp', 'kvp'), may hold values from -0.0625 to 0.0625
- norm_gain: bfloat16 [8192], P('kvp'), may hold values from 0.25 to 1.75
- gate_weight: bfloat16 [8192, 28672], P('kvp', 'tp'), may hold values from -0.0625 to 0.0625
- up_weight: bfloat16 [8192, 28672], P('kvp', 'tp'), may hold values from -0.0625 to 0.0625
- down_weight: bfloat16 [28672, 8192], P('tp', 'kvp'), may hold values from -0.03125 to 0.03125
Outputs:
- attended: bfloat16 [8, 8192], P(None, 'tp')
- layer_out: float32 [8, 8192], P(None, 'kvp')
Inputs may be any that keep to these rules, and one draw needn't show every extreme that they name: Row s is a permutation of 0 to 31; the page of request b's block j in KV shard s is s * 32 + block_table[s, b * 4 + j]. The lengths sum to 81920 and the longest is exactly 16384.
All inputs are finite; a program needn't handle non-finite values.
Results may differ from a plain program's by a relative error of at most 0.0056.
Values may be sent and summed in bfloat16 or wider, within the bound.
A program may use at most 64 MiB of HBM per device.

v0:
```python
import functools

import jax
import jax.numpy as jnp
from jax import lax
from jax.sharding import Mesh
from jax.sharding import PartitionSpec as P

D = 8192
HD = 128
KVP = ("kvp_0", "kvp_1")


def gathered_once(value, axis):
    leaves = jax.tree.leaves(value)
    order = sorted(range(len(leaves)), key=lambda k: -leaves[k].size)
    width = (1, *leaves[order[0]].shape)[-1]
    lines = [
        jnp.pad(leaves[k].reshape(-1), (0, -leaves[k].size % width)).reshape(-1, width)
        for k in order
    ]
    both, at, found = (lax.all_gather(jnp.concatenate(lines), axis), 0, {})
    for k, line in zip(order, lines):
        piece = both[:, at : at + len(line)].reshape(len(both), -1)
        found[k] = piece[:, : leaves[k].size].reshape(-1, *leaves[k].shape)
        at += len(line)
    numbers = iter(range(len(leaves)))
    return jax.tree.map(lambda _: found[next(numbers)], value)


def joined_all(value, axes, combine):
    for axis in axes:
        pieces = gathered_once(value, axis)
        value = jax.tree.map(lambda part: part[0], pieces)
        for k in range(1, lax.axis_size(axis)):
            value = combine(value, jax.tree.map(lambda part: part[k], pieces))
    return value


def sent_to_all(value, axis):
    copies = jnp.broadcast_to(value, (lax.axis_size(axis), *value.shape))
    return lax.all_to_all(copies, axis, split_axis=0, concat_axis=0, tiled=True)


def taken_together(value, axis):
    everything = sent_to_all(value, axis)
    return jnp.sum(everything, axis=0)


def by_axis(value, axes):
    return functools.reduce(lax.psum, axes, value)


def cut_along(value, dim, devices):
    before, after = (value.shape[:dim], value.shape[dim + 1 :])
    return jnp.moveaxis(value.reshape(*before, devices, -1, *after), dim, 0)


def sent_and_summed(value, axis, dim):
    devices = lax.axis_size(axis)
    tiles = lax.all_to_all(cut_along(value, dim, devices), axis, 0, 0, tiled=True)
    return jnp.sum(tiles, axis=0)


def sent_together(arrays, axis, dim, along):
    widths = [a.shape[along] for a in arrays]
    both = jnp.concatenate(arrays, axis=along)
    result = sent_and_summed(both, axis, dim)
    return tuple(jnp.split(result, [sum(widths[:k]) for k in range(1, len(widths))], axis=along))


def joined_along(tiles, dim):
    tiles = jnp.moveaxis(tiles, 0, dim)
    dims = tiles.shape
    return tiles.reshape(*dims[:dim], dims[dim] * dims[dim + 1], *dims[dim + 2 :])


def collect(value, axis, dim):
    tiles = sent_to_all(value, axis)
    return joined_along(tiles, dim)


def combine(earlier, later):
    peak_early, sum_early, out_early = earlier
    peak_late, sum_late, out_late = later
    row_peak = jnp.maximum(peak_early, peak_late)
    factor_early = jnp.exp(peak_early - row_peak)
    factor_late = jnp.exp(peak_late - row_peak)
    weight_sum = sum_early * factor_early + sum_late * factor_late
    out_sum = out_early * factor_early[..., None] + out_late * factor_late[..., None]
    return (row_peak, weight_sum, out_sum)


def body(
    queries,
    key_pool,
    value_pool,
    block_table,
    lengths,
    residual_in,
    out_weight,
    norm_gain,
    gate_weight,
    up_weight,
    down_weight,
):
    requests = queries.shape[0]
    kv_local = key_pool.shape[2] // HD
    heads_local = queries.shape[1] // HD
    group_size = heads_local // kv_local
    blocks = block_table.shape[1] // requests
    shard_span = blocks * key_pool.shape[1]
    shard_index = lax.axis_index(KVP)
    page_ids = block_table[0].reshape(requests, blocks)
    key_rows = key_pool[page_ids].reshape(requests, shard_span, kv_local, HD)
    value_rows = value_pool[page_ids].reshape(requests, shard_span, kv_local, HD)
    query_heads = queries.reshape(requests, kv_local, group_size, HD)
    scores = jnp.einsum(
        "bkgd,btkd->bkgt", query_heads, key_rows, preferred_element_type=jnp.float32
    ) * HD ** (-0.5)
    positions = shard_index * shard_span + jnp.arange(shard_span, dtype=jnp.int32)
    is_live = (positions[None, :] < lengths[:, None])[:, None, None, :]
    masked = jnp.where(is_live, scores, -1e30)
    row_peak = jnp.max(masked, axis=-1)
    weights = jnp.where(is_live, jnp.exp(masked - row_peak[..., None]), 0.0)
    weight_sum = jnp.sum(weights, axis=-1).reshape(requests, heads_local)
    rounded = weights.astype(jnp.bfloat16)
    out_sum = jnp.einsum("bkgt,btkd->bkgd", rounded, value_rows, preferred_element_type=jnp.float32)
    out_sum = out_sum.reshape(requests, heads_local, HD)
    row_peak = row_peak.reshape(requests, heads_local)
    row_peak, weight_sum, out_sum = joined_all((row_peak, weight_sum, out_sum), KVP, combine)
    attended = (
        (out_sum / weight_sum[..., None]).astype(jnp.bfloat16).reshape(requests, heads_local * HD)
    )
    projected = jnp.dot(attended, out_weight, preferred_element_type=jnp.float32)
    mixed = residual_in + taken_together(projected, "tp")
    squares = by_axis(jnp.sum(mixed * mixed, axis=1), KVP)
    inv_rms = lax.rsqrt(squares / D + 0.1)
    normed = (mixed * inv_rms[:, None] * norm_gain.astype(jnp.float32)).astype(jnp.bfloat16)
    gate_part = jnp.dot(normed, gate_weight, preferred_element_type=jnp.float32)
    up_part = jnp.dot(normed, up_weight, preferred_element_type=jnp.float32)
    gate_share, up_share = sent_together((gate_part, up_part), KVP, 1, 0)
    hidden_share = (jax.nn.silu(gate_share) * up_share).astype(jnp.bfloat16)
    down_part = jnp.dot(
        collect(hidden_share, KVP, 1), down_weight, preferred_element_type=jnp.float32
    )
    layer_out = mixed + taken_together(down_part, "tp")
    return (attended, layer_out)


def solution(mesh):
    finer = Mesh(mesh.devices.reshape(16, 4, mesh.shape["tp"]), ("kvp_0", "kvp_1", "tp"))
    placed = (
        P(None, "tp"),
        P(KVP, None, "tp"),
        P(KVP, None, "tp"),
        P(KVP, None),
        P(),
        P(None, KVP),
        P("tp", KVP),
        P(KVP),
        P(KVP, "tp"),
        P(KVP, "tp"),
        P("tp", KVP),
    )
    return jax.shard_map(
        body, mesh=finer, in_specs=placed, out_specs=(P(None, "tp"), P(None, KVP)), check_vma=False
    )
```

profile of v0, /device:TPU:1, one launch (start us, length us, event | category | flops | bytes accessed | tf_op | source)
XLA Modules:
  0.0 168.1 jit_solution(15688187760744057415)
XLA Ops:
  0.7 0.5 broadcast.150
  1.4 0.7 reduce.39
  2.2 0.6 copy-done.8
  3.0 1.7 %gather_fusion = bf16[32,64,128]{2,1,0:T(8,128)(2,1)S(1)} fusion(bf16[32,64,128]{2,1,0:T(8,128)(2,1)} %param.12, s32[1024]{0:T(1024)S(1)} %pad_clamp_fusion), kind=kCustom, calls=%fused_computation | custom fusion | bytes 1048704 | tf_op jit(solution)/shard_map/gather | solution.py:115
  4.7 0.3 fusion.136
  5.4 0.4 copy-done.3
  5.7 0.6 gather_fusion.1
  6.6 32.1 %all-gather.2 = f32[16,66,128]{2,1,0:T(8,128)S(1)} all-gather(f32[1,66,128]{2,1,0:T(8,128)S(1)} %maximum_bitcast_fusion), channel_id=2, replica_groups=mesh['kvp_0'=16,'kvp_1'=4,'tp'=8] {'kvp_0'}, dimensions={0}, use_global_device_ids=true | all-gather | bytes 574464 | tf_op jit(solution)/shard_map/all_gather | solution.py:22
  38.9 0.3 fusion.6
  39.3 9.7 %all-gather.3 = f32[4,66,128]{2,1,0:T(8,128)S(1)} all-gather(f32[1,66,128]{2,1,0:T(8,128)S(1)} %maximum_bitcast_fusion.1), channel_id=3, replica_groups=mesh['kvp_0'=16,'kvp_1'=4,'tp'=8] {'kvp_1'}, dimensions={0}, use_global_device_ids=true | all-gather | bytes 168960 | tf_op jit(solution)/shard_map/all_gather | solution.py:22
  50.8 0.5 copy-done.5
  51.2 19.9 %all_to_all.20 = f32[8,8,128]{2,1,0:T(8,128)S(1)} all-to-all(f32[8,8,128]{2,1,0:T(8,128)S(1)} %broadcast_in_dim.30), channel_id=1, replica_groups=mesh['kvp_0'=16,'kvp_1'=4,'tp'=8] {'tp'}, dimensions={0} | all-to-all | bytes 65536 | tf_op jit(solution)/shard_map/all_to_all | solution.py:42
  71.3 20.1 %psum.14 = f32[8]{0:T(128)S(1)} all-reduce(f32[8]{0:T(128)S(1)} %get-tuple-element.10), channel_id=1, replica_groups=mesh['kvp_0'=16,'kvp_1'=4,'tp'=8] {'kvp_0'}, use_global_device_ids=true, to_apply=%region_4.5 | all-reduce | flops 8 | bytes 64 | tf_op jit(solution)/shard_map/psum | solution.py:51
  91.4 8.2 %psum.15 = f32[8]{0:T(128)S(1)} all-reduce(f32[8]{0:T(128)S(1)} %psum.14), channel_id=1, replica_groups=mesh['kvp_0'=16,'kvp_1'=4,'tp'=8] {'kvp_1'}, use_global_device_ids=true, to_apply=%region_5.6 | all-reduce | flops 8 | bytes 64 | tf_op jit(solution)/shard_map/psum | solution.py:51
  100.2 0.4 reshape.1487
  100.7 0.3 copy.47
  101.0 0.5 reshape.1568
  101.5 25.3 %all_to_all.21 = f32[64,1,896]{2,1,0:T(1,128)S(1)} all-to-all(f32[64,1,896]{2,1,0:T(1,128)S(1)} %reshape.1568), channel_id=1, replica_groups=mesh['kvp_0'=16,'kvp_1'=4,'tp'=8] {'kvp_0','kvp_1'}, dimensions={0} | all-to-all | bytes 458752 | tf_op jit(solution)/shard_map/all_to_all | solution.py:61
  126.8 0.5 broadcast.151
  127.3 1.2 reduce.40
  128.5 0.4 reshape.1569
  129.2 18.0 %all_to_all.22 = bf16[64,2,224]{2,1,0:T(2,128)(2,1)S(1)} all-to-all(bf16[64,2,224]{2,1,0:T(2,128)(2,1)S(1)} %reshape.1570), channel_id=1, replica_groups=mesh['kvp_0'=16,'kvp_1'=4,'tp'=8] {'kvp_0','kvp_1'}, dimensions={0} | all-to-all | bytes 114688 | tf_op jit(solution)/shard_map/all_to_all | solution.py:42
  147.8 19.6 %all_to_all.23 = f32[8,8,128]{2,1,0:T(8,128)S(1)} all-to-all(f32[8,8,128]{2,1,0:T(8,128)S(1)} %broadcast_in_dim.32), channel_id=1, replica_groups=mesh['kvp_0'=16,'kvp_1'=4,'tp'=8] {'tp'}, dimensions={0} | all-to-all | bytes 65536 | tf_op jit(solution)/shard_map/all_to_all | solution.py:42
  167.5 0.6 add.245
  (81 shorter events, 4.6 us)
Async XLA Ops:
  0.6 99.0 %copy-start = (bf16[128,3584]{1,0:T(8,128)(2,1)S(1)}, bf16[128,3584]{1,0:T(8,128)(2,1)}, u32[]{:S(2)}) copy-start(bf16[128,3584]{1,0:T(8,128)(2,1)} %param.19) | copy-start | bytes 2752516
  0.7 0.7 copy-start.9
  2.2 0.7 copy-start.8
  3.0 1.7 %copy-start.6 = (bf16[8,1024]{1,0:T(8,128)(2,1)S(1)}, bf16[8,1024]{1,0:T(8,128)(2,1)}, u32[]{:S(2)}) copy-start(bf16[8,1024]{1,0:T(8,128)(2,1)} %param.11) | copy-start | bytes 49156
  4.7 1.0 copy-start.3
  49.7 1.0 copy-start.4
  50.2 21.0 %copy-start.7 = (f32[8,128]{1,0:T(8,128)S(1)}, f32[8,128]{1,0:T(8,128)}, u32[]{:S(2)}) copy-start(f32[8,128]{1,0:T(8,128)} %param.16) | copy-start | bytes 12292
  50.2 41.2 %copy-start.10 = (bf16[128]{0:T(256)(128)(2,1)S(1)}, bf16[128]{0:T(256)(128)(2,1)}, u32[]{:S(2)}) copy-start(bf16[128]{0:T(256)(128)(2,1)} %param.18) | copy-start | bytes 772
  50.2 49.7 %copy-start.1 = (bf16[128,3584]{1,0:T(8,128)(2,1)S(1)}, bf16[128,3584]{1,0:T(8,128)(2,1)}, u32[]{:S(2)}) copy-start(bf16[128,3584]{1,0:T(8,128)(2,1)} %param.20) | copy-start | bytes 2752516
  50.6 0.6 copy-start.5
  128.9 18.7 %copy-start.2 = (bf16[3584,128]{1,0:T(8,128)(2,1)S(1)}, bf16[3584,128]{1,0:T(8,128)(2,1)}, u32[]{:S(2)}) copy-start(bf16[3584,128]{1,0:T(8,128)(2,1)} %param.21) | copy-start | bytes 2752516
where the time goes:
time: 168 us
  blocking collectives  153 us (91%)
  local copies, waits for them, and re-layouts  9.11 us (5%)
  other arithmetic  3.59 us (2%)
    all_to_all x3, blocking collectives, sent_to_all(): return lax.all_to_all(copies, axis, split_axis=0, concat_axis=0, tiled=True)  57.6 us
    all_gather x2, blocking collectives, gathered_once(): both, at, found = (lax.all_gather(jnp.concatenate(lines), axis), 0, {})  41.8 us
    psum x2, blocking collectives, by_axis(): return functools.reduce(lax.psum, axes, value)  28.3 us
    all_to_all x1, blocking collectives, sent_and_summed(): lax.all_to_all(cut_along(value, dim, devices), axis, 0, 0, tiled=True)  25.3 us
    unnamed x27, local copies, waits for them, and re-layouts  3.68 us

commit v1 on v0

v1 whole, which is shorter than its diff:
```python
import jax
import jax.numpy as jnp
from jax import lax
from jax.experimental import pallas as pl
from jax.experimental.pallas import tpu as pltpu
from jax.sharding import PartitionSpec as P

MESH = pl.DeviceIdType.MESH
F32 = jnp.float32
BF16 = jnp.bfloat16

NY, NZ, NT = 4, 16, 8
B, HD = 8, 128
D = 8192
HL = 8
BLOCKS = 4
PAGE = 64
SPAN = BLOCKS * PAGE
TILES = 7
QUARTER = TILES * 128
UNITS = 2 * TILES
FAR_FIRST = (8, 7, 9, 6, 10, 5, 11, 4, 12, 3, 13, 2, 14, 1, 15)


def iota(shape, dim):
    return lax.broadcasted_iota(jnp.int32, shape, dim)


def kernel(
    q_h, k_h, v_h, tab_h, len_h, res_h, wo_h, gain_h, wg_h, wu_h, wd_h,
    att_h, lay_h,
    q_v, k_v, v_v, tab_s, len_s, res_v, wo_v, gain_v, wg_v, wu_v, wd_v,
    osend, stsend, yo, yst, zo, zst, attb, attv, tp1, sqy, sqz, sqsend,
    ysend, yrecv, units, zrecv, hidz, yh, tp2, layv,
    lsem, osem, yo_s, yo_r, yst_s, yst_r, zo_s, zo_r, zst_s, zst_r, ya_s, ya_r,
    t1_s, t1_r, sy_s, sy_r, sz_s, sz_r, yr_s, yr_r, zr_s, zr_r, za_s, za_r,
    yh_s, yh_r, t2_s, t2_r,
):
    kv = lax.axis_index("kvp")
    tp = lax.axis_index("tp")
    z = lax.div(kv, NY)
    y = lax.rem(kv, NY)

    def ypos(d):
        return lax.rem(y + d, NY)

    def zpos(d):
        return lax.rem(z + d, NZ)

    def ydev(d):
        return (z * NY + ypos(d), tp)

    def zdev(d):
        return (zpos(d) * NY + y, tp)

    def tdev(d):
        return (kv, lax.rem(tp + d, NT))

    barrier = pltpu.get_barrier_semaphore()
    partners = (
        [zdev(d) for d in FAR_FIRST]
        + [tdev(d) for d in range(1, NT)]
        + [ydev(d) for d in range(1, NY)]
    )
    for dev in partners:
        pl.semaphore_signal(barrier, inc=1, device_id=dev, device_id_type=MESH)

    loads = []

    def load(src, dst):
        copy = pltpu.make_async_copy(src, dst, lsem.at[len(loads)])
        copy.start()
        loads.append(copy)
        return copy

    l_tab = load(tab_h, tab_s)
    l_len = load(len_h, len_s)
    l_q = load(q_h, q_v)
    l_k = [load(k_h.at[pl.ds(8 * i, 8)], k_v.at[pl.ds(8 * i, 8)]) for i in range(4)]
    l_v = [load(v_h.at[pl.ds(8 * i, 8)], v_v.at[pl.ds(8 * i, 8)]) for i in range(4)]
    l_res = load(res_h, res_v)
    l_gain = load(gain_h, gain_v)
    l_wo = load(wo_h, wo_v)
    l_w = []
    for d in range(NY):
        cols = pl.ds(pl.multiple_of(ypos(d) * QUARTER, 128), QUARTER)
        l_w.append((load(wg_h.at[:, cols], wg_v.at[d]), load(wu_h.at[:, cols], wu_v.at[d])))
    l_wd = []
    for d in range(NY):
        rows = pl.ds(pl.multiple_of(ypos(d) * QUARTER, 128), QUARTER)
        l_wd.append(load(wd_h.at[rows, :], wd_v.at[d]))

    sent = []

    def send(src, dst, ssem, rsem, dev):
        copy = pltpu.make_async_remote_copy(
            src_ref=src, dst_ref=dst, send_sem=ssem, recv_sem=rsem, device_id=dev, device_id_type=MESH
        )
        copy.start()
        return copy

    def arrived(dst, ssem, rsem, dev):
        pltpu.make_async_remote_copy(
            src_ref=dst, dst_ref=dst, send_sem=ssem, recv_sem=rsem, device_id=dev, device_id_type=MESH
        ).wait_recv()

    def left(copies):
        for copy in copies:
            copy.wait_send()

    l_tab.wait()
    l_len.wait()
    l_q.wait()
    qf = q_v[...].astype(F32)
    q_rows = jnp.concatenate([qf[:, h * HD : (h + 1) * HD] for h in range(HL)], axis=0).astype(BF16)
    request = iota((HL * B, SPAN), 0) & (B - 1)
    position = iota((HL * B, SPAN), 1) + kv * SPAN
    length = jnp.full((HL * B, SPAN), len_s[0], jnp.int32)
    for b in range(1, B):
        length = jnp.where(request == b, len_s[b], length)
    live = position < length
    for copy in l_k:
        copy.wait()
    scores = None
    for b in range(B):
        keys = jnp.concatenate([k_v[tab_s[0, b * BLOCKS + j]] for j in range(BLOCKS)], axis=0)
        part = lax.dot_general(q_rows, keys, (((1,), (1,)), ((), ())), preferred_element_type=F32)
        scores = part if scores is None else jnp.where(request == b, part, scores)
    masked = jnp.where(live, scores * HD ** (-0.5), -1e30)
    peak = jnp.max(masked, axis=1, keepdims=True)
    weights = jnp.where(live, jnp.exp(masked - peak), 0.0)
    total = jnp.sum(weights, axis=1, keepdims=True)
    for copy in l_v:
        copy.wait()
    out = None
    for b in range(B):
        values = jnp.concatenate([v_v[tab_s[0, b * BLOCKS + j]] for j in range(BLOCKS)], axis=0)
        mine = jnp.where(request == b, weights, 0.0).astype(BF16)
        part = jnp.dot(mine, values, preferred_element_type=F32)
        out = part if out is None else out + part
    out = out.astype(BF16).reshape(NY, 2, B, HD)

    row16 = iota((16, 128), 0)
    lane16 = iota((16, 128), 1)
    diag = row16 == lane16
    diag_up = row16 + 16 == lane16
    osend[...] = out
    for j in range(NY):
        rows = slice(16 * j, 16 * j + 16)
        spread = jnp.where(diag, peak[rows], 0.0) + jnp.where(diag_up, total[rows], 0.0)
        stsend[j] = jnp.sum(spread, axis=0, keepdims=True)

    pl.semaphore_wait(barrier, len(partners))

    copies = []
    for d in (2, 1, 3):
        j = ypos(d)
        copies.append(send(stsend.at[j], yst.at[NY - d], yst_s.at[d], yst_r.at[NY - d], ydev(d)))
        copies.append(send(osend.at[j], yo.at[NY - d], yo_s.at[d], yo_r.at[NY - d], ydev(d)))
    yo[0] = osend[y]
    yst[0] = stsend[y]
    for k in range(1, NY):
        arrived(yst.at[k], yst_s.at[k], yst_r.at[k], ydev(k))
        arrived(yo.at[k], yo_s.at[k], yo_r.at[k], ydev(k))

    def as_column(line):
        return jnp.sum(jnp.where(diag, line, 0.0), axis=1, keepdims=True)

    stats = jnp.concatenate([yst[k] for k in range(NY)], axis=0)
    peak = jnp.max(stats, axis=0, keepdims=True)
    factor = jnp.exp(stats - peak)
    total = jnp.sum(factor * pltpu.roll(stats, 112, 1), axis=0, keepdims=True)
    mixed_out = None
    for k in range(NY):
        part = as_column(factor[k : k + 1]) * yo[k].astype(F32).reshape(16, HD)
        mixed_out = part if mixed_out is None else mixed_out + part
    lane1 = iota((1, 128), 1)
    zo[z] = mixed_out.astype(BF16).reshape(2, B, HD)
    zst[z] = jnp.where(lane1 < 16, peak, jnp.where(lane1 < 32, pltpu.roll(total, 16, 1), 0.0))

    zcopies = []
    for d in FAR_FIRST:
        zcopies.append(send(zst.at[z], zst.at[z], zst_s.at[d], zst_r.at[NZ - d], zdev(d)))
        zcopies.append(send(zo.at[z], zo.at[z], zo_s.at[d], zo_r.at[NZ - d], zdev(d)))
    left(copies)
    for d in range(1, NZ):
        arrived(zst.at[zpos(d)], zst_s.at[d], zst_r.at[d], zdev(d))
    stats = jnp.concatenate([zst[k] for k in range(NZ)], axis=0)
    peak = jnp.max(stats, axis=0, keepdims=True)
    factor = jnp.exp(stats - peak)
    total = jnp.sum(factor * pltpu.roll(stats, 112, 1), axis=0, keepdims=True)
    share = factor / total
    columns = [as_column(share[k : k + 1]) for k in range(NZ)]
    for d in range(1, NZ):
        arrived(zo.at[zpos(d)], zo_s.at[d], zo_r.at[d], zdev(d))
    att = None
    for k in range(NZ):
        part = columns[k] * zo[k].astype(F32).reshape(16, HD)
        att = part if att is None else att + part
    pair = pl.ds(2 * y, 2)
    attb[pair] = att.astype(BF16).reshape(2, B, HD)

    copies = [send(attb.at[pair], attb.at[pair], ya_s.at[d], ya_r.at[NY - d], ydev(d)) for d in (2, 1, 3)]
    left(zcopies)
    l_wo.wait()
    for k in range(1, NY):
        theirs = pl.ds(2 * ypos(k), 2)
        arrived(attb.at[theirs], ya_s.at[k], ya_r.at[k], ydev(k))
    for h in range(HL):
        attv[:, h * HD : (h + 1) * HD] = attb[h]

    tp1[tp] = jnp.dot(attv[...], wo_v[...], preferred_element_type=F32)
    tcopies = [
        send(tp1.at[tp], tp1.at[tp], t1_s.at[d], t1_r.at[NT - d], tdev(d)) for d in (4, 5, 3, 2, 6, 7, 1)
    ]
    att_copy = pltpu.make_async_copy(attv, att_h, osem.at[0])
    att_copy.start()
    left(copies)
    l_res.wait()
    l_gain.wait()
    for k in range(1, NT):
        arrived(tp1.at[lax.rem(tp + k, NT)], t1_s.at[k], t1_r.at[k], tdev(k))
    shared = tp1[0]
    for k in range(1, NT):
        shared = shared + tp1[k]
    mixed = res_v[...] + shared

    row8 = iota((B, 128), 0)
    lane8 = iota((B, 128), 1)
    squares = jnp.sum(mixed * mixed, axis=1, keepdims=True)
    sqy[0] = jnp.sum(jnp.where(row8 == lane8, squares, 0.0), axis=0, keepdims=True)
    scaled = (mixed * gain_v[...].astype(F32)).astype(BF16)
    copies = [send(sqy.at[0], sqy.at[NY - d], sy_s.at[d], sy_r.at[NY - d], ydev(d)) for d in (2, 1, 3)]

    def gate_up(d):
        l_w[d][0].wait()
        l_w[d][1].wait()
        gate = jnp.dot(scaled, wg_v[d], preferred_element_type=F32)
        up = jnp.dot(scaled, wu_v[d], preferred_element_type=F32)
        return [a[:, t * 128 : (t + 1) * 128] for a in (gate, up) for t in range(TILES)]

    for d in (2, 1, 3):
        parts = gate_up(d)
        for i in range(2 * TILES):
            ysend[d, i] = parts[i].astype(BF16)
        copies.append(send(ysend.at[d], yrecv.at[NY - d], yr_s.at[d], yr_r.at[NY - d], ydev(d)))
    parts = gate_up(0)
    for k in range(1, NY):
        arrived(sqy.at[k], sy_s.at[k], sy_r.at[k], ydev(k))
    sqz[0] = (sqy[0] + sqy[1]) + (sqy[2] + sqy[3])
    for d in FAR_FIRST:

        @pl.when(zpos(d) < UNITS)
        def _():
            send(sqz.at[0], sqz.at[NZ - d], sz_s.at[d], sz_r.at[NZ - d], zdev(d))

    left(tcopies)
    for k in range(1, NY):
        arrived(yrecv.at[k], yr_s.at[k], yr_r.at[k], ydev(k))
        for i in range(2 * TILES):
            parts[i] = parts[i] + yrecv[k, i].astype(F32)
    low = row8 < 4
    for t in range(TILES):
        gate, up = parts[t], parts[TILES + t]
        units[2 * t] = jnp.where(low, gate, pltpu.roll(up, 4, 0)).astype(BF16)
        units[2 * t + 1] = jnp.where(low, pltpu.roll(gate, 4, 0), up).astype(BF16)

    for d in FAR_FIRST:

        @pl.when(zpos(d) < UNITS)
        def _():
            send(units.at[zpos(d)], zrecv.at[NZ - d], zr_s.at[d], zr_r.at[NZ - d], zdev(d))

    left(copies)

    @pl.when(z < UNITS)
    def _():
        half = lax.rem(z, 2)
        for k in range(1, NZ):
            arrived(sqz.at[k], sz_s.at[k], sz_r.at[k], zdev(k))
        squares = sqz[0]
        for k in range(1, NZ):
            squares = squares + sqz[k]
        wanted = lane8 == (row8 & 3) + 4 * half
        column = jnp.sum(jnp.where(wanted, squares, 0.0), axis=1, keepdims=True)
        inv_rms = lax.rsqrt(column / D + 0.1)
        own = units[z].astype(F32)
        for k in range(1, NZ):
            arrived(zrecv.at[k], zr_s.at[k], zr_r.at[k], zdev(k))
            own = own + zrecv[k].astype(F32)
        own = own * inv_rms
        hidden = own / (1.0 + jnp.exp(-own)) * pltpu.roll(own, 4, 0)
        placed = jnp.where(half == 0, hidden, pltpu.roll(hidden, 4, 0))
        mine = lax.shift_right_logical(row8, 2) == half
        hidz[z] = jnp.where(mine, placed, 0.0).astype(BF16)
        for d in FAR_FIRST:
            send(hidz.at[z], hidz.at[z], za_s.at[d], za_r.at[NZ - d], zdev(d))

    for d in range(1, NZ):

        @pl.when(zpos(d) < UNITS)
        def _():
            arrived(hidz.at[zpos(d)], za_s.at[d], za_r.at[d], zdev(d))

    for t in range(TILES):
        yh[0, t] = hidz[2 * t] + hidz[2 * t + 1]
    copies = [send(yh.at[0], yh.at[NY - d], yh_s.at[d], yh_r.at[NY - d], ydev(d)) for d in (2, 1, 3)]

    def down(k):
        l_wd[k].wait()
        rows = jnp.concatenate([yh[k, t] for t in range(TILES)], axis=1)
        return jnp.dot(rows, wd_v[k], preferred_element_type=F32)

    part = down(0)
    for k in (1, 3, 2):
        arrived(yh.at[k], yh_s.at[k], yh_r.at[k], ydev(k))
        part = part + down(k)
    tp2[tp] = part
    tcopies = [
        send(tp2.at[tp], tp2.at[tp], t2_s.at[d], t2_r.at[NT - d], tdev(d)) for d in (4, 5, 3, 2, 6, 7, 1)
    ]
    left(copies)
    for d in range(1, NZ):

        @pl.when(zpos(d) < UNITS)
        def _():
            pltpu.make_async_remote_copy(
                sqz.at[0], sqz.at[0], sz_s.at[d], sz_r.at[d], zdev(d), MESH
            ).wait_send()
            pltpu.make_async_remote_copy(
                units.at[0], units.at[0], zr_s.at[d], zr_r.at[d], zdev(d), MESH
            ).wait_send()

    @pl.when(z < UNITS)
    def _():
        for d in range(1, NZ):
            pltpu.make_async_remote_copy(
                hidz.at[0], hidz.at[0], za_s.at[d], za_r.at[d], zdev(d), MESH
            ).wait_send()

    att_copy.wait()
    for k in range(1, NT):
        arrived(tp2.at[lax.rem(tp + k, NT)], t2_s.at[k], t2_r.at[k], tdev(k))
    shared = tp2[0]
    for k in range(1, NT):
        shared = shared + tp2[k]
    layv[...] = mixed + shared
    lay_copy = pltpu.make_async_copy(layv, lay_h, osem.at[1])
    lay_copy.start()
    left(tcopies)
    lay_copy.wait()


def body(queries, key_pool, value_pool, block_table, lengths, residual_in, out_weight, norm_gain,
         gate_weight, up_weight, down_weight):
    vm = pltpu.VMEM
    dma = pltpu.SemaphoreType.DMA
    scratch = [
        vm((B, HL * HD), BF16), vm((32, PAGE, HD), BF16), vm((32, PAGE, HD), BF16),
        pltpu.SMEM((1, 32), jnp.int32), pltpu.SMEM((B,), jnp.int32), vm((B, 128), F32),
        vm((HL * HD, 128), BF16), vm((1, 128), BF16),
        vm((NY, 128, QUARTER), BF16), vm((NY, 128, QUARTER), BF16), vm((NY, QUARTER, 128), BF16),
        vm((NY, 2, B, HD), BF16), vm((NY, 1, 128), F32),
        vm((NY, 2, B, HD), BF16), vm((NY, 1, 128), F32),
        vm((NZ, 2, B, HD), BF16), vm((NZ, 1, 128), F32),
        vm((HL, B, HD), BF16), vm((B, HL * HD), BF16), vm((NT, B, 128), F32),
        vm((NY, 1, 128), F32), vm((NZ, 1, 128), F32), vm((1, 128), F32),
        vm((NY, 2 * TILES, B, 128), BF16), vm((NY, 2 * TILES, B, 128), BF16),
        vm((NZ, B, 128), BF16), vm((NZ, B, 128), BF16), vm((UNITS, B, 128), BF16),
        vm((NY, TILES, B, 128), BF16), vm((NT, B, 128), F32), vm((B, 128), F32),
        dma((32,)), dma((2,)),
        dma((NY,)), dma((NY,)), dma((NY,)), dma((NY,)),
        dma((NZ,)), dma((NZ,)), dma((NZ,)), dma((NZ,)),
        dma((NY,)), dma((NY,)), dma((NT,)), dma((NT,)),
        dma((NY,)), dma((NY,)), dma((NZ,)), dma((NZ,)),
        dma((NY,)), dma((NY,)), dma((NZ,)), dma((NZ,)),
        dma((NZ,)), dma((NZ,)), dma((NY,)), dma((NY,)), dma((NT,)), dma((NT,)),
    ]
    anywhere = pl.BlockSpec(memory_space=pl.ANY)
    return pl.pallas_call(
        kernel,
        out_shape=(
            jax.ShapeDtypeStruct((B, HL * HD), BF16),
            jax.ShapeDtypeStruct((B, 128), F32),
        ),
        in_specs=[anywhere] * 11,
        out_specs=(anywhere, anywhere),
        scratch_shapes=scratch,
        compiler_params=pltpu.CompilerParams(collective_id=0, has_side_effects=True),
        name="layer",
    )(queries, key_pool, value_pool, block_table, lengths, residual_in, out_weight,
      norm_gain.reshape(1, 128), gate_weight, up_weight, down_weight)


def solution(mesh):
    placed = (
        P(None, "tp"), P("kvp", None, "tp"), P("kvp", None, "tp"), P("kvp", None), P(),
        P(None, "kvp"), P("tp", "kvp"), P("kvp"), P("kvp", "tp"), P("kvp", "tp"), P("tp", "kvp"),
    )
    return jax.shard_map(
        body, mesh=mesh, in_specs=placed, out_specs=(P(None, "tp"), P(None, "kvp")), check_vma=False
    )
```

time: 168 us -> 64.7 us (0.39)
  blocking collectives: 153 us -> 0 us
  Pallas kernels: 0 us -> 61.9 us
  local copies, waits for them, and re-layouts: 9.11 us -> 1.92 us
  other arithmetic: 3.59 us -> 0 us
    all_to_all x4 -> x0, blocking collectives: 82.9 us -> none  [the longest x3 57.6 us: sent_to_all(): return lax.all_to_all(copies, axis, split_axis=0, concat_axis=0, tiled=True)]
    pallas_call x0 -> x1, Pallas kernels: none -> 61.9 us  [body(): pl.pallas_call(kernel, out_shape=(jax.ShapeDtypeStruct((B, HL * HD), BF16...]
    all_gather x2 -> x0, blocking collectives: 41.8 us -> none  [gathered_once(): both, at, found = (lax.all_gather(jnp.concatenate(lines), axis), 0, {})]
    psum x2 -> x0, blocking collectives: 28.3 us -> none  [by_axis(): return functools.reduce(lax.psum, axes, value)]
    gather x2 -> x0, local copies, waits for them, and re-layouts: 2.35 us -> none  [the longest x1 1.7 us: body(): key_rows = key_pool[page_ids].reshape(requests, shard_span, kv_local, HD)]
    unnamed x27 -> x4, local copies, waits for them, and re-layouts: 3.68 us -> 1.92 us
where the time goes in v1:
time: 64.7 us; the launch traced here: 64.5 us
  Pallas kernels  61.9 us (96%)
  local copies, waits for them, and re-layouts  1.92 us (3%)
  between operations  0.65 us (1%)
    pallas_call x1, Pallas kernels, body(): pl.pallas_call(kernel, out_shape=(jax.ShapeDtypeStruct((B, HL * HD), BF16...  61.9 us
    unnamed x4, local copies, waits for them, and re-layouts  1.92 us

profile of v1, /device:TPU:1, one launch (start us, length us, event | category | flops | bytes accessed | tf_op | source)
XLA Modules:
  0.0 64.5 jit_solution(7347634895854150583)
XLA Ops:
  0.6 61.9 %layer.1 = (bf16[8,1024]{1,0:T(8,128)(2,1)}, f32[8,128]{1,0:T(8,128)}) custom-call(bf16[8,1024]{1,0:T(8,128)(2,1)} %q_h.1, bf16[32,64,128]{2,1,0:T(8,128)(2,1)} %k_h.1, bf16[32,64,128]{2,1,0:T(8,128)(2,1)} %v_h.1, s32[1,32]{1,0:T(1,128)} %tab_h.1, s32[8]{0:T(128)} %len_h.1, f32[8,128]{1,0:T(8,128)} %res_h.1, bf16[1024,128]{1,0:T(8,128)(2,1)} %wo_h.1, ...), custom_call_target="tpu_custom_call" | custom-call | tf_op jit(solution)/shard_map/layer/pallas_call | solution.py:380
  62.6 0.0 copy-start
  62.6 1.3 %copy.15 = bf16[8,1024]{1,0:T(8,128)(2,1)} copy(bf16[8,1024]{1,0:T(8,128)(2,1)} %get-tuple-element.4) | data formatting | bytes 32768
  63.9 0.0 copy-done
  63.9 0.6 copy.16
Async XLA Ops:
  62.6 1.3 %copy-start = (f32[8,128]{1,0:T(8,128)S(1)}, f32[8,128]{1,0:T(8,128)}, u32[]{:S(2)}) copy-start(f32[8,128]{1,0:T(8,128)} %get-tuple-element.5) | copy-start | bytes 12292
